TPU v7x, 32 devices: a whole 2x2x4 slice. The times are simulated.
32 devices in a mesh: worker: 8 (over y, x, core), mp: 4 (over z).
Axes of the slice: x: 2, y: 2, z: 4, core: 2. Of those that a mesh axis runs over, the one named last changes fastest.
Arguments:
- gradients: float32 [8, 2097152], P('worker', 'mp'), may hold values from -100 to 100
- neighbours: int32 [8, 3], replicated, may hold values from 0 to 7, as said below
- winner: int32 [1], replicated, may hold values from 0 to 7
Outputs:
- scores: float32 [8], replicated
- aggregate: float32 [2097152], P(('mp', 'worker'))
Inputs may be any that keep to these rules, and one draw needn't show every extreme that they name: `neighbours`: row i lists 3 different workers, none of them equal to i.
All inputs are finite; a program needn't handle non-finite values.
Results may differ from a plain program's by a relative error of at most 0.0003.
Values may be sent and summed in bfloat16 or wider, within the bound.
No kernel may reach another device: no remote copies, remote signals or barrier semaphores. Data moves between devices by JAX's collectives and lax.ppermute only.
A program may use at most 64 MiB of HBM per device.

v0:
```python
import jax
import jax.numpy as jnp
from jax import lax
from jax.sharding import PartitionSpec as P


def from_root(block, axis, holder):
    block = jnp.where(lax.axis_index(axis) == holder, block, jnp.zeros_like(block))
    return lax.psum(block, axis)


def body(gradients, neighbours, winner):
    rounded = gradients.astype(jnp.bfloat16)
    workers = lax.axis_size("worker")
    own_index = lax.axis_index("worker")
    length = gradients.shape[1]
    columns = lax.all_to_all(rounded, "worker", split_axis=1, concat_axis=0, tiled=True)
    partial_value = lax.dot_general(
        columns, columns, (((1,), (1,)), ((), ())), preferred_element_type=jnp.float32
    )
    gram_matrix = lax.psum(partial_value, ("worker", "mp"))
    squares = jnp.diagonal(gram_matrix)
    distance = squares[:, None] + squares[None, :] - 2.0 * gram_matrix
    counts = jnp.sum(
        (neighbours[:, :, None] == jnp.arange(workers, dtype=jnp.int32)[None, None, :]).astype(
            jnp.float32
        ),
        axis=1,
    )
    total_entries = neighbours.shape[1] * length * lax.axis_size("mp")
    scores = jnp.sum(counts * distance, axis=1) / jnp.float32(total_entries)
    piece_length = length // workers
    selected = from_root(gradients[0], "worker", winner[0])
    aggregate = lax.dynamic_slice_in_dim(selected, own_index * piece_length, piece_length, 0)
    return (scores, aggregate)


def solution(mesh):
    in_specs = (P("worker", "mp"), P(), P())
    out_specs = (P(), P(("mp", "worker")))
    return jax.shard_map(body, mesh=mesh, in_specs=in_specs, out_specs=out_specs, check_vma=False)
```

profile of v0, /device:TPU:0, one launch (start us, length us, event | category | flops | bytes accessed | tf_op | source)
XLA Modules:
  0.0 107.3 jit_solution(818342998343869056)
XLA Ops:
  7.8 6.5 %broadcast_select_fusion = (f32[1,524288]{1,0:T(1,128)}, bf16[1,524288]{1,0:T(2,128)(2,1)S(1)}) fusion(f32[1,524288]{1,0:T(1,128)} %param.3, pred[]{:T(512)S(6)} %eq.19), kind=kLoop, calls=%fused_computation.1 | loop fusion | flops 1048576 | bytes 5242881 | tf_op jit(solution)/shard_map/jit(_where)/select_n | solution.py:8
  14.3 0.5 broadcast.34
  14.8 7.0 %reduce = bf16[8,65536]{1,0:T(8,128)(2,1)S(1)} reduce(bf16[8,1,65536]{2,1,0:T(2,128)(2,1)S(1)} %bitcast.12, bf16[]{:T(256)} %broadcast.34), dimensions={1}, to_apply=%bitcast.8.reduce_sub_computation | reduce | bytes 2097154
  21.9 1.9 %reshape.22 = bf16[8,2,32768]{2,1,0:T(2,128)(2,1)} reshape(bf16[8,65536]{1,0:T(8,128)(2,1)S(1)} %reduce) | data formatting | bytes 2097152
  23.7 0.0 copy-start
  23.7 5.3 %all-to-all-start = ((bf16[8,2,32768]{2,1,0:T(2,128)(2,1)}), bf16[8,2,32768]{2,1,0:T(2,128)(2,1)S(1)}, u32[]{:S(2)}, u32[]{:S(2)}) async-start(bf16[8,2,32768]{2,1,0:T(2,128)(2,1)} %reshape.22), calls=%async_computation | async-start | bytes 2097152 | tf_op jit(solution)/shard_map/all_to_all | solution.py:17
  29.1 0.0 all-reduce.2.cloned.1.call-start
  29.1 0.7 all-reduce.2.cloned.1.call-update
  29.8 0.0 copy-done
  29.8 0.1 convert_reduce_fusion
  29.9 16.4 %all-to-all-done = bf16[8,2,32768]{2,1,0:T(2,128)(2,1)S(1)} async-done(((bf16[8,2,32768]{2,1,0:T(2,128)(2,1)}), bf16[8,2,32768]{2,1,0:T(2,128)(2,1)S(1)}, u32[]{:S(2)}, u32[]{:S(2)}) %all-to-all-start) | async-done | bytes 1048608 | tf_op jit(solution)/shard_map/all_to_all | solution.py:17
  46.3 1.0 reshape.23
  47.3 1.2 %fusion = f32[8,8]{1,0:T(8,128)S(1)} fusion(bf16[1,8,65536]{2,0,1:T(2,128)(2,1)S(1)} %bitcast.13), kind=kOutput, calls=%fused_computation.2 | convolution fusion | flops 8388608 | bytes 1048832 | tf_op jit(solution)/shard_map/dot_general | solution.py:18
  48.5 39.8 %psum.14 = f32[8,8]{1,0:T(8,128)S(1)} all-reduce(f32[8,8]{1,0:T(8,128)S(1)} %fusion), channel_id=1, replica_groups=mesh['worker'=8,'mp'=4] {'worker','mp'}, use_global_device_ids=true, to_apply=%region_1.2 | all-reduce | flops 64 | bytes 512 | tf_op jit(solution)/shard_map/psum | solution.py:21
  88.3 0.6 gather_fusion
  88.9 0.2 multiply_reduce_fusion
  89.1 0.5 broadcast_multiply_fusion
  89.6 9.1 %all-reduce.2.cloned.1.call-done = f32[524288]{0:T(1024)} async-done(((f32[524288]{0:T(1024)}), f32[524288]{0:T(1024)}) %all-reduce.2.cloned.1.call-update) | async-done | bytes 2097168 | tf_op jit(solution)/shard_map/psum | solution.py:9
  98.8 1.7 %dynamic_slice.3 = f32[65536]{0:T(1024)} dynamic-slice(f32[524288]{0:T(1024)} %all-reduce.2.cloned.1.call-done, s32[]{:T(128)S(6)} %select_n.21), dynamic_slice_sizes={65536} | dynamic-slice | bytes 524292 | tf_op jit(solution)/shard_map/dynamic_slice | solution.py:34
  (1 shorter events, 0.0 us)
Async XLA Ops:
  23.7 6.1 %copy-start = (s32[8,3]{0,1:T(4,128)S(1)}, s32[8,3]{0,1:T(4,128)}, u32[]{:S(2)}) copy-start(s32[8,3]{0,1:T(4,128)} %param.4) | copy-start | bytes 292
  23.7 22.5 %all-to-all-start = ((bf16[8,2,32768]{2,1,0:T(2,128)(2,1)}), bf16[8,2,32768]{2,1,0:T(2,128)(2,1)S(1)}, u32[]{:S(2)}, u32[]{:S(2)}) async-start(bf16[8,2,32768]{2,1,0:T(2,128)(2,1)} %reshape.22), calls=%async_computation | async-start | bytes 2097152 | tf_op jit(solution)/shard_map/all_to_all | solution.py:17
  29.1 69.7 %all-reduce.2.cloned.1.call-start = ((), (), s32[]{:S(2)}) async-start(), calls=%async_computation.1 | async-start | bytes 4194304 | tf_op jit(solution)/shard_map/psum | solution.py:9
Sparse Core Ops, SparseCore 0:
  33.1 65.6 all-reduce.1
where the time goes:
time: 108 us; the launch traced here: 107 us
  blocking collectives  39.8 us (37%)
  waiting for transfers between devices  26.2 us (24%)
  between operations  14.7 us (14%)
  other arithmetic  14.3 us (13%)
  local copies, waits for them, and re-layouts  5.71 us (5%)
  starting transfers between devices  5.37 us (5%)
  matrix products  1.2 us (1%)
    psum x1, blocking collectives, body(): gram_matrix = lax.psum(partial_value, ('worker', 'mp'))  39.8 us
    all_to_all x1, waiting for transfers between devices, body(): lax.all_to_all(rounded, 'worker', split_axis=1, concat_axis=0, tiled=True)  16.4 us
    psum x1, waiting for transfers between devices, from_root(): return lax.psum(block, axis)  9.12 us
    unnamed x1, other arithmetic  7.03 us
    select_n x1, other arithmetic, from_root(): jnp.where(lax.axis_index(axis) == holder, block, jnp.zeros_like(block))  6.5 us
    all_to_all x1, starting transfers between devices, body(): lax.all_to_all(rounded, 'worker', split_axis=1, concat_axis=0, tiled=True)  5.33 us
    unnamed x5, local copies, waits for them, and re-layouts  3.41 us
  transfers between devices with their start and end apart: 2, of which 2 were waited for; matrix products, arithmetic and copies ran while one was open for 3% of the time, Pallas kernels for 0%

commit v1 on v0

--- a/solution.py
+++ b/solution.py
@@ -18,7 +18,7 @@
     partial_value = lax.dot_general(
         columns, columns, (((1,), (1,)), ((), ())), preferred_element_type=jnp.float32
     )
-    gram_matrix = lax.psum(partial_value, ("worker", "mp"))
+    gram_matrix = jnp.sum(lax.all_gather(partial_value, ("worker", "mp")), axis=0)
     squares = jnp.diagonal(gram_matrix)
     distance = squares[:, None] + squares[None, :] - 2.0 * gram_matrix
     counts = jnp.sum(

time: 108 us -> 126 us (1.17)
  blocking collectives: 39.8 us -> 67.3 us
  waiting for transfers between devices: 26.2 us -> 17 us
    all_gather x0 -> x1, blocking collectives: none -> 67.3 us  [body(): lax.all_gather(partial_value, ('worker', 'mp'))]
    psum x1 -> x0, blocking collectives: 39.8 us -> none  [body(): gram_matrix = lax.psum(partial_value, ('worker', 'mp'))]
    psum x1, waiting for transfers between devices: 9.12 us -> 0.01 us  [from_root(): return lax.psum(block, axis)]
  transfers between devices with their start and end apart: 2 -> 2, of which waited for: 2 -> 1; matrix products, arithmetic and copies ran while one was open for 3% -> 3% of each run, Pallas kernels for 0% -> 0%
where the time goes in v1:
time: 126 us
  blocking collectives  67.3 us (53%)
  waiting for transfers between devices  17 us (13%)
  between operations  14.7 us (12%)
  other arithmetic  14.3 us (11%)
  local copies, waits for them, and re-layouts  5.71 us (5%)
  starting transfers between devices  5.37 us (4%)
    all_gather x1, blocking collectives, body(): lax.all_gather(partial_value, ('worker', 'mp'))  67.3 us
    all_to_all x1, waiting for transfers between devices, body(): lax.all_to_all(rounded, 'worker', split_axis=1, concat_axis=0, tiled=True)  16.4 us
    unnamed x1, other arithmetic  7.03 us
    select_n x1, other arithmetic, from_root(): jnp.where(lax.axis_index(axis) == holder, block, jnp.zeros_like(block))  6.49 us
    all_to_all x1, starting transfers between devices, body(): lax.all_to_all(rounded, 'worker', split_axis=1, concat_axis=0, tiled=True)  5.33 us
    unnamed x5, local copies, waits for them, and re-layouts  3.41 us
  transfers between devices with their start and end apart: 2, of which 1 were waited for; matrix products, arithmetic and copies ran while one was open for 3% of the time, Pallas kernels for 0%

profile of v1, /device:TPU:0, one launch (start us, length us, event | category | flops | bytes accessed | tf_op | source)
XLA Modules:
  0.0 125.7 jit_solution(11120278656684225482)
XLA Ops:
  7.8 6.5 %broadcast_select_fusion = (f32[1,524288]{1,0:T(1,128)}, bf16[1,524288]{1,0:T(2,128)(2,1)S(1)}) fusion(f32[1,524288]{1,0:T(1,128)} %param.3, pred[]{:T(512)S(6)} %eq.19), kind=kLoop, calls=%fused_computation.1 | loop fusion | flops 1048576 | bytes 5242881 | tf_op jit(solution)/shard_map/jit(_where)/select_n | solution.py:8
  14.3 0.5 broadcast.34
  14.8 7.0 %reduce = bf16[8,65536]{1,0:T(8,128)(2,1)S(1)} reduce(bf16[8,1,65536]{2,1,0:T(2,128)(2,1)S(1)} %bitcast.14, bf16[]{:T(256)} %broadcast.34), dimensions={1}, to_apply=%bitcast.10.reduce_sub_computation | reduce | bytes 2097154
  21.9 1.9 %reshape.23 = bf16[8,2,32768]{2,1,0:T(2,128)(2,1)} reshape(bf16[8,65536]{1,0:T(8,128)(2,1)S(1)} %reduce) | data formatting | bytes 2097152
  23.7 0.0 copy-start
  23.7 5.3 %all-to-all-start = ((bf16[8,2,32768]{2,1,0:T(2,128)(2,1)}), bf16[8,2,32768]{2,1,0:T(2,128)(2,1)S(1)}, u32[]{:S(2)}, u32[]{:S(2)}) async-start(bf16[8,2,32768]{2,1,0:T(2,128)(2,1)} %reshape.23), calls=%async_computation | async-start | bytes 2097152 | tf_op jit(solution)/shard_map/all_to_all | solution.py:17
  29.1 0.0 all-reduce.2.cloned.1.call-start
  29.1 0.7 all-reduce.2.cloned.1.call-update
  29.8 0.0 copy-done
  29.8 0.1 convert_reduce_fusion
  29.9 16.4 %all-to-all-done = bf16[8,2,32768]{2,1,0:T(2,128)(2,1)S(1)} async-done(((bf16[8,2,32768]{2,1,0:T(2,128)(2,1)}), bf16[8,2,32768]{2,1,0:T(2,128)(2,1)S(1)}, u32[]{:S(2)}, u32[]{:S(2)}) %all-to-all-start) | async-done | bytes 1048608 | tf_op jit(solution)/shard_map/all_to_all | solution.py:17
  46.2 1.0 reshape.24
  47.3 1.2 fusion
  48.5 67.3 %all-gather = f32[256,8]{1,0:T(8,128)S(1)} all-gather(f32[8,8]{1,0:T(8,128)S(1)} %fusion), channel_id=2, replica_groups=mesh['worker'=8,'mp'=4] {'worker','mp'}, dimensions={0}, use_global_device_ids=true | all-gather | bytes 8448 | tf_op jit(solution)/shard_map/all_gather | solution.py:21
  115.8 0.6 gather_fusion
  116.5 0.2 multiply_reduce_fusion
  116.7 0.5 broadcast_multiply_fusion
  117.2 0.0 all-reduce.2.cloned.1.call-done
  117.2 1.7 %dynamic_slice.3 = f32[65536]{0:T(1024)} dynamic-slice(f32[524288]{0:T(1024)} %all-reduce.2.cloned.1.call-done, s32[]{:T(128)S(6)} %select_n.21), dynamic_slice_sizes={65536} | dynamic-slice | bytes 524292 | tf_op jit(solution)/shard_map/dynamic_slice | solution.py:34
  (2 shorter events, 0.0 us)
Async XLA Ops:
  23.7 6.1 %copy-start = (s32[8,3]{0,1:T(4,128)S(1)}, s32[8,3]{0,1:T(4,128)}, u32[]{:S(2)}) copy-start(s32[8,3]{0,1:T(4,128)} %param.4) | copy-start | bytes 292
  23.7 22.5 %all-to-all-start = ((bf16[8,2,32768]{2,1,0:T(2,128)(2,1)}), bf16[8,2,32768]{2,1,0:T(2,128)(2,1)S(1)}, u32[]{:S(2)}, u32[]{:S(2)}) async-start(bf16[8,2,32768]{2,1,0:T(2,128)(2,1)} %reshape.23), calls=%async_computation | async-start | bytes 2097152 | tf_op jit(solution)/shard_map/all_to_all | solution.py:17
  29.1 88.1 %all-reduce.2.cloned.1.call-start = ((), (), s32[]{:S(2)}) async-start(), calls=%async_computation.1 | async-start | bytes 4194304 | tf_op jit(solution)/shard_map/psum | solution.py:9
Sparse Core Ops, SparseCore 0:
  33.1 65.4 all-reduce.1
